TPU v7x, 32 devices: a whole 2x2x4 slice. The times are simulated.
32 devices in a mesh: beam: 2 (over x), pulse: 16 (over z, y, core).
Axes of the slice: x: 2, y: 2, z: 4, core: 2. Of those that a mesh axis runs over, the one named last changes fastest.
Arguments:
- echoes: float32 [2, 4096, 1536], P(None, 'pulse', 'beam'), parts along dimension 2, may hold values from -6 to 6
- guard_gates: int32 [1], replicated, may hold values from 1 to 4
- train_gates: int32 [1], replicated, may hold values from 4 to 16
Outputs:
- powers: float32 [4096, 1536], P('pulse', 'beam'), parts along dimension 1
- statistic: float32 [4096, 1536], P('pulse', 'beam'), parts along dimension 1
There are 2 independent parts, one for each index of `beam`. A program takes and returns all parts, laid end to end along the dimension named above; an argument that names none is the same for every part. Nothing has to cross between parts.
All inputs are finite; a program needn't handle non-finite values.
Results may differ from a plain program's by a relative error of at most 0.0003.
Values sent between devices are 32-bit elements; how exact they have to be, the bound alone decides.
A program may use at most 192 MiB of HBM per device.

v0:
```python
import jax
import jax.numpy as jnp
from jax import lax
from jax.sharding import PartitionSpec as P

PULSES = 4096
GUARD_BINS = 2
TRAIN_BINS = 4


TWO_PI = 6.283185307179586


def padded_2(cells, sides, width):
    for axis, dim in sides:
        count = lax.axis_size(axis)
        head = lax.slice_in_dim(cells, 0, width, axis=dim)
        tail = lax.slice_in_dim(cells, cells.shape[dim] - width, cells.shape[dim], axis=dim)
        cells = jnp.concatenate(
            [
                lax.ppermute(tail, axis, [(i, (i + 1) % count) for i in range(count)]),
                cells,
                lax.ppermute(head, axis, [((i + 1) % count, i) for i in range(count)]),
            ],
            axis=dim,
        )
    return cells


def small_tables(count):
    index_row = jnp.arange(count, dtype=jnp.int32)
    phases = (index_row[:, None] * index_row[None, :] % count).astype(jnp.float32) * (
        TWO_PI / count
    )
    return (jnp.cos(phases), jnp.sin(phases))


def product(left, right):
    return jnp.dot(left, right, precision=lax.Precision.HIGHEST, preferred_element_type=jnp.float32)


def factored_powers(samples):
    width = samples.shape[2]
    bit_count = PULSES.bit_length() - 1
    first_radix = 2 ** (bit_count // 2)
    second_radix = PULSES // first_radix
    cos_first, sin_first = small_tables(first_radix)
    real_in = samples[0].reshape(first_radix, second_radix * width)
    imag_in = samples[1].reshape(first_radix, second_radix * width)
    real_one = (product(cos_first, real_in) + product(sin_first, imag_in)).reshape(
        first_radix, second_radix, width
    )
    imag_one = (product(cos_first, imag_in) - product(sin_first, real_in)).reshape(
        first_radix, second_radix, width
    )
    first_ids = jnp.arange(first_radix, dtype=jnp.int32)
    second_ids = jnp.arange(second_radix, dtype=jnp.int32)
    twist = (first_ids[:, None] * second_ids[None, :] % PULSES).astype(jnp.float32) * (
        TWO_PI / PULSES
    )
    twist_cos = jnp.cos(twist)[:, :, None]
    twist_sin = jnp.sin(twist)[:, :, None]
    real_two = twist_cos * real_one + twist_sin * imag_one
    imag_two = twist_cos * imag_one - twist_sin * real_one
    real_two = jnp.transpose(real_two, (1, 0, 2)).reshape(second_radix, first_radix * width)
    imag_two = jnp.transpose(imag_two, (1, 0, 2)).reshape(second_radix, first_radix * width)
    cos_second, sin_second = small_tables(second_radix)
    scale_factor = 1.0 / jnp.sqrt(jnp.float32(PULSES))
    real_out = (product(cos_second, real_two) + product(sin_second, imag_two)) * scale_factor
    imag_out = (product(cos_second, imag_two) - product(sin_second, real_two)) * scale_factor
    result = real_out * real_out + imag_out * imag_out
    return result.reshape(PULSES, width)


def shards(echoes, guard_gates, train_gates):
    devices_count = lax.axis_size("pulse")
    bins_local = PULSES // devices_count
    gates_count = echoes.shape[2]
    columns = factored_powers(
        lax.all_to_all(echoes, "pulse", split_axis=2, concat_axis=1, tiled=True)
    )
    powers = lax.all_to_all(columns, "pulse", split_axis=0, concat_axis=1, tiled=True)
    reach = GUARD_BINS + TRAIN_BINS
    padded = padded_2(powers, (("pulse", 0),), reach)
    doppler_sum = jnp.zeros_like(powers)
    for shift_bins in range(GUARD_BINS + 1, reach + 1):
        above = padded[reach + shift_bins : reach + shift_bins + bins_local]
        below = padded[reach - shift_bins : reach - shift_bins + bins_local]
        doppler_sum = doppler_sum + above + below
    guard_width = guard_gates[0]
    train_width = train_gates[0]
    gate_ids = jnp.arange(gates_count, dtype=jnp.int32)
    offsets = jnp.abs(gate_ids[:, None] - gate_ids[None, :])
    band = ((offsets > guard_width) & (offsets <= guard_width + train_width)).astype(jnp.float32)
    range_sum = jnp.dot(
        powers, band, precision=lax.Precision.HIGHEST, preferred_element_type=jnp.float32
    )
    range_count = jnp.sum(band, axis=0)
    noise_level = (range_sum + doppler_sum) / (range_count[None, :] + 2.0 * TRAIN_BINS)
    statistic = powers / (noise_level + 1.0)
    return (powers, statistic)


def solution(mesh):
    return jax.shard_map(
        shards,
        mesh=mesh,
        in_specs=(P(None, "pulse", "beam"), P(), P()),
        out_specs=(P("pulse", "beam"), P("pulse", "beam")),
        check_vma=False,
    )
```

profile of v0, /device:TPU:0, one launch (start us, length us, event | category | flops | bytes accessed | tf_op | source)
XLA Modules:
  0.0 128.5 jit_solution(2452970888408496449)
XLA Ops:
  0.6 3.7 %copy.33 = f32[2,256,768]{1,0,2:T(2,128)} copy(f32[2,256,768]{2,1,0:T(8,128)} %param.3) | data formatting | bytes 3145728 | tf_op args[0]
  4.3 7.4 %all-to-all-start = ((f32[2,256,768]{1,0,2:T(2,128)}), f32[2,256,768]{1,0,2:T(2,128)S(1)}, u32[]{:S(2)}, u32[]{:S(2)}) async-start(f32[2,256,768]{1,0,2:T(2,128)} %copy.33), calls=%async_computation | async-start | bytes 3145728 | tf_op jit(solution)/shard_map/all_to_all | solution.py:80
  11.9 31.7 %all-to-all-done = f32[2,256,768]{1,0,2:T(2,128)S(1)} async-done(((f32[2,256,768]{1,0,2:T(2,128)}), f32[2,256,768]{1,0,2:T(2,128)S(1)}, u32[]{:S(2)}, u32[]{:S(2)}) %all-to-all-start) | async-done | bytes 1572896 | tf_op jit(solution)/shard_map/all_to_all | solution.py:80
  43.7 1.0 fusion.84
  44.7 0.6 copy.36
  45.3 1.8 %reshape_squeeze.7 = f32[64,3072]{1,0:T(8,128)S(1)} reshape(f32[1,16,256,48]{3,2,1,0:T(8,128)S(1)} %copy.36) | data formatting | bytes 1572864 | tf_op jit(solution)/shard_map/reshape;squeeze | solution.py:49
  47.1 1.8 %fusion.44 = f32[64,3072]{1,0:T(8,128)} fusion(f32[64,3072]{1,0:T(8,128)S(1)} %reshape_squeeze.7), kind=kOutput, calls=%fused_computation.66 | convolution fusion | flops 151052288 | bytes 1572864 | tf_op jit(solution)/shard_map/dot_general | solution.py:39
  48.9 1.7 %copy.35 = f32[1,16,256,48]{3,2,1,0:T(8,128)S(1)} copy(f32[1,16,256,48]{2,3,1,0:T(8,128)} %get-tuple-element.10) | data formatting | bytes 1572864 | tf_op jit(solution)/shard_map/slice | solution.py:48
  50.6 2.7 %reshape_squeeze.6 = f32[64,3072]{1,0:T(8,128)} reshape(f32[1,16,256,48]{3,2,1,0:T(8,128)S(1)} %copy.35) | data formatting | bytes 1572864 | tf_op jit(solution)/shard_map/reshape;squeeze | solution.py:48
  53.3 3.0 %fusion.46 = f32[64,3072]{1,0:T(8,128)} fusion(f32[64,3072]{1,0:T(8,128)} %reshape_squeeze.6), kind=kOutput, calls=%fused_computation.67 | convolution fusion | flops 151052288 | bytes 1572864 | tf_op jit(solution)/shard_map/dot_general | solution.py:39
  56.4 1.8 %convolution_subtract_fusion.1 = f32[64,3072]{1,0:T(8,128)} fusion(f32[64,3072]{1,0:T(8,128)S(1)} %copy-done.2, f32[64,3072]{1,0:T(8,128)S(1)} %copy-done), kind=kOutput, calls=%fused_computation.2 | convolution fusion | flops 151248896 | bytes 2359296 | tf_op jit(solution)/shard_map/dot_general | solution.py:39
  58.2 2.0 %reshape.68 = f32[64,64,48]{2,1,0:T(8,128)S(1)} reshape(f32[64,3072]{1,0:T(8,128)} %convolution_subtract_fusion.1) | data formatting | bytes 1572864 | tf_op jit(solution)/shard_map/reshape | solution.py:53
  60.2 2.9 %convolution_add_fusion.1 = f32[64,3072]{1,0:T(8,128)} fusion(f32[64,3072]{1,0:T(8,128)} %fusion.46, f32[64,3072]{1,0:T(8,128)S(1)} %reshape_squeeze.7), kind=kOutput, calls=%fused_computation.3 | convolution fusion | flops 151248896 | bytes 2359296 | tf_op jit(solution)/shard_map/dot_general | solution.py:39
  63.1 3.1 %reshape.67 = f32[64,64,48]{2,1,0:T(8,128)} reshape(f32[64,3072]{1,0:T(8,128)} %convolution_add_fusion.1) | data formatting | bytes 1572864 | tf_op jit(solution)/shard_map/reshape | solution.py:50
  66.2 4.2 %subtract_bitcast_fusion = (f32[64,64,48]{2,0,1:T(8,128)}, f32[64,64,48]{2,0,1:T(8,128)S(1)}) fusion(f32[64,64,48]{2,1,0:T(8,128)} %reshape.67, f32[64,64,48]{2,1,0:T(8,128)S(1)} %reshape.68, f32[64,64]{1,0:T(8,128)S(1)} %get-tuple-element.14, f32[64,64]{1,0:T(8,128)S(1)} %get-tuple-element.15), kind=kLoop, calls=%fused_computation.14 | loop fusion | flops 1179648 | bytes 3178496 | tf_op jit(solution)/shard_map/transpose | solution.py:66
  70.5 1.2 copy.37
  71.7 1.8 %reshape.69 = f32[64,3072]{1,0:T(8,128)S(1)} reshape(f32[64,64,48]{2,1,0:T(8,128)S(1)} %copy.37) | data formatting | bytes 1572864 | tf_op jit(solution)/shard_map/reshape | solution.py:65
  73.4 1.8 %fusion.42 = f32[64,3072]{1,0:T(8,128)} fusion(f32[64,3072]{1,0:T(8,128)S(1)} %reshape.69), kind=kOutput, calls=%fused_computation.65 | convolution fusion | flops 151052288 | bytes 1572864 | tf_op jit(solution)/shard_map/dot_general | solution.py:39
  75.3 2.8 %copy.38 = f32[64,64,48]{2,1,0:T(8,128)S(1)} copy(f32[64,64,48]{2,0,1:T(8,128)} %get-tuple-element.8) | data formatting | bytes 1572864 | tf_op jit(solution)/shard_map/transpose | solution.py:66
  78.1 2.7 %reshape.70 = f32[64,3072]{1,0:T(8,128)} reshape(f32[64,64,48]{2,1,0:T(8,128)S(1)} %copy.38) | data formatting | bytes 1572864 | tf_op jit(solution)/shard_map/reshape | solution.py:66
  80.7 2.2 %fusion.40 = f32[64,3072]{1,0:T(8,128)S(1)} fusion(f32[64,3072]{1,0:T(8,128)} %reshape.70), kind=kOutput, calls=%fused_computation.64 | convolution fusion | flops 151052288 | bytes 1572864 | tf_op jit(solution)/shard_map/dot_general | solution.py:39
  82.9 1.0 fusion.1
  83.9 1.0 fusion.4
  84.9 0.9 all_to_all.28
  85.8 1.5 %copy.39 = f32[16,256,48]{1,2,0:T(8,128)} copy(f32[16,256,48]{2,1,0:T(8,128)S(1)} %all_to_all.28) | data formatting | bytes 1572864 | tf_op jit(solution)/shard_map/all_to_all | solution.py:82
  87.2 9.1 %all-to-all-start.1 = ((f32[16,256,48]{1,2,0:T(8,128)}), f32[16,256,48]{1,2,0:T(8,128)S(1)}, u32[]{:S(2)}, u32[]{:S(2)}) async-start(f32[16,256,48]{1,2,0:T(8,128)} %copy.39), calls=%async_computation.1 | async-start | bytes 1572864 | tf_op jit(solution)/shard_map/all_to_all | solution.py:82
  97.7 0.6 convert_reduce_fusion
  98.3 16.8 %all-to-all-done.1 = f32[16,256,48]{1,2,0:T(8,128)S(1)} async-done(((f32[16,256,48]{1,2,0:T(8,128)}), f32[16,256,48]{1,2,0:T(8,128)S(1)}, u32[]{:S(2)}, u32[]{:S(2)}) %all-to-all-start.1) | async-done | bytes 786464 | tf_op jit(solution)/shard_map/all_to_all | solution.py:82
  115.4 4.0 %collective-permute-start = (f32[6,768]{1,0:T(8,128)S(1)}, f32[6,768]{1,0:T(8,128)S(1)}, u32[]{:S(2)}, u32[]{:S(2)}) collective-permute-start(f32[6,768]{1,0:T(8,128)S(1)} %copy.46), channel_id=1, source_target_pairs={{1,0},{2,1},{3,2},{4,3},{5,4},{6,5},{7,6},{8,7},{9,8},{10,9},{11,1... | collective-permute-start | bytes 55304 | tf_op jit(solution)/shard_map/ppermute | solution.py:23
  119.9 1.0 collective-permute-done
  120.9 4.6 %collective-permute-done.1 = f32[6,768]{1,0:T(8,128)S(1)} collective-permute-done((f32[6,768]{1,0:T(8,128)S(1)}, f32[6,768]{1,0:T(8,128)S(1)}, u32[]{:S(2)}, u32[]{:S(2)}) %collective-permute-start.1) | collective-permute-done | bytes 18464 | tf_op jit(solution)/shard_map/ppermute | solution.py:21
  125.5 3.0 %add_divide_fusion = f32[256,768]{1,0:T(8,128)} fusion(f32[256,768]{1,0:T(8,128)S(1)} %copy.45, f32[6,768]{1,0:T(8,128)S(1)} %collective-permute-done.1, f32[6,768]{1,0:T(8,128)S(1)} %collective-permute-done, f32[768]{0:T(1024)S(1)} %broadcast_add_fusion, f32[256,768]{0,1:T(8,128)S(1)} %bitcast.33, s32[]{:T(128)S(6)} %add.101, s32[]{:T(128)} %bitcast.27), kind=kOutput, calls=%fused_computation.42 | convolution fusion | flops 1818624000 | bytes 2399240 | tf_op jit(solution)/shard_map/dot_general | solution.py:95
  (18 shorter events, 1.0 us)
Async XLA Ops:
  4.3 39.3 %all-to-all-start = ((f32[2,256,768]{1,0,2:T(2,128)}), f32[2,256,768]{1,0,2:T(2,128)S(1)}, u32[]{:S(2)}, u32[]{:S(2)}) async-start(f32[2,256,768]{1,0,2:T(2,128)} %copy.33), calls=%async_computation | async-start | bytes 3145728 | tf_op jit(solution)/shard_map/all_to_all | solution.py:80
  53.3 3.0 %copy-start = (f32[64,3072]{1,0:T(8,128)S(1)}, f32[64,3072]{1,0:T(8,128)}, u32[]{:S(2)}) copy-start(f32[64,3072]{1,0:T(8,128)} %reshape_squeeze.6) | copy-start | bytes 2359300
  53.3 3.0 %copy-start.2 = (f32[64,3072]{1,0:T(8,128)S(1)}, f32[64,3072]{1,0:T(8,128)}, u32[]{:S(2)}) copy-start(f32[64,3072]{1,0:T(8,128)} %fusion.44) | copy-start | bytes 2359300
  80.7 2.2 %copy-start.1 = (f32[64,3072]{1,0:T(8,128)S(1)}, f32[64,3072]{1,0:T(8,128)}, u32[]{:S(2)}) copy-start(f32[64,3072]{1,0:T(8,128)} %reshape.70) | copy-start | bytes 2359300
  80.7 2.2 %copy-start.3 = (f32[64,3072]{1,0:T(8,128)S(1)}, f32[64,3072]{1,0:T(8,128)}, u32[]{:S(2)}) copy-start(f32[64,3072]{1,0:T(8,128)} %fusion.42) | copy-start | bytes 2359300
  87.2 27.8 %all-to-all-start.1 = ((f32[16,256,48]{1,2,0:T(8,128)}), f32[16,256,48]{1,2,0:T(8,128)S(1)}, u32[]{:S(2)}, u32[]{:S(2)}) async-start(f32[16,256,48]{1,2,0:T(8,128)} %copy.39), calls=%async_computation.1 | async-start | bytes 1572864 | tf_op jit(solution)/shard_map/all_to_all | solution.py:82
  115.4 5.5 %collective-permute-start = (f32[6,768]{1,0:T(8,128)S(1)}, f32[6,768]{1,0:T(8,128)S(1)}, u32[]{:S(2)}, u32[]{:S(2)}) collective-permute-start(f32[6,768]{1,0:T(8,128)S(1)} %copy.46), channel_id=1, source_target_pairs={{1,0},{2,1},{3,2},{4,3},{5,4},{6,5},{7,6},{8,7},{9,8},{10,9},{11,1... | collective-permute-start | bytes 55304 | tf_op jit(solution)/shard_map/ppermute | solution.py:23
  119.5 6.0 %collective-permute-start.1 = (f32[6,768]{1,0:T(8,128)S(1)}, f32[6,768]{1,0:T(8,128)S(1)}, u32[]{:S(2)}, u32[]{:S(2)}) collective-permute-start(f32[6,768]{1,0:T(8,128)S(1)} %copy.47), channel_id=1, source_target_pairs={{0,1},{1,2},{2,3},{3,4},{4,5},{5,6},{6,7},{7,8},{8,9},{9,10},{10,1... | collective-permute-start | bytes 55304 | tf_op jit(solution)/shard_map/ppermute | solution.py:21
  119.8 8.7 %copy-start.4 = (f32[256,768]{1,0:T(8,128)}, f32[256,768]{1,0:T(8,128)S(1)}, u32[]{:S(2)}) copy-start(f32[256,768]{1,0:T(8,128)S(1)} %copy.45) | copy-start | bytes 2359300
where the time goes:
time: 129 us
  waiting for transfers between devices  54.1 us (42%)
  local copies, waits for them, and re-layouts  28.2 us (22%)
  starting transfers between devices  20.6 us (16%)
  matrix products  18.6 us (14%)
  other arithmetic  5 us (4%)
  between operations  2.08 us (2%)
    all_to_all x1, waiting for transfers between devices, shards(): lax.all_to_all(echoes, 'pulse', split_axis=2, concat_axis=1, tiled=True)  31.7 us
    all_to_all x1, waiting for transfers between devices, shards(): lax.all_to_all(columns, 'pulse', split_axis=0, concat_axis=1, tiled=True)  16.8 us
    dot_general x8, matrix products, product(): jnp.dot(left, right, precision=lax.Precision.HIGHEST, preferred_element_t...  15.5 us
    all_to_all x1, starting transfers between devices, shards(): lax.all_to_all(columns, 'pulse', split_axis=0, concat_axis=1, tiled=True)  9.12 us
    all_to_all x1, starting transfers between devices, shards(): lax.all_to_all(echoes, 'pulse', split_axis=2, concat_axis=1, tiled=True)  7.41 us
    ppermute x1, waiting for transfers between devices, padded_2(): lax.ppermute(tail, axis, [(i, (i + 1) % count) for i in range(count)])  4.6 us
    transpose x1, other arithmetic, factored_powers(): jnp.transpose(imag_two, (1, 0, 2))  4.25 us
    ppermute x1, starting transfers between devices, padded_2(): lax.ppermute(head, axis, [((i + 1) % count, i) for i in range(count)])  4.02 us
  transfers between devices with their start and end apart: 4, of which 4 were waited for; matrix products, arithmetic and copies ran while one was open for 1% of the time, Pallas kernels for 0%

commit v1 on v0

--- a/solution.py
+++ b/solution.py
@@ -1,6 +1,11 @@
+import functools
+
 import jax
 import jax.numpy as jnp
+import numpy as np
 from jax import lax
+from jax.experimental import pallas as pl
+from jax.experimental.pallas import tpu as pltpu
 from jax.sharding import PartitionSpec as P
 
 PULSES = 4096
@@ -72,7 +77,7 @@
     return result.reshape(PULSES, width)
 
 
-def shards(echoes, guard_gates, train_gates):
+def generic_shards(echoes, guard_gates, train_gates):
     devices_count = lax.axis_size("pulse")
     bins_local = PULSES // devices_count
     gates_count = echoes.shape[2]
@@ -101,6 +106,266 @@
     return (powers, statistic)
 
 
+LANES = 128
+ROWS = 8
+HIGHEST = lax.Precision.HIGHEST
+
+
+def butterflies(cells):
+    count = len(cells)
+    if count == 1:
+        return cells
+    even = butterflies(cells[0::2])
+    odd = butterflies(cells[1::2])
+    low, high = [], []
+    for k in range(count // 2):
+        re, im = odd[k]
+        if 4 * k == count:
+            re, im = im, -re
+        elif k:
+            c, s = np.cos(2 * np.pi * k / count), np.sin(2 * np.pi * k / count)
+            c, s = np.float32(c), np.float32(s)
+            re, im = c * re + s * im, c * im - s * re
+        low.append((even[k][0] + re, even[k][1] + im))
+        high.append((even[k][0] - re, even[k][1] - im))
+    return low + high
+
+
+def swap_digits(rows, width):
+    count = len(rows)
+    lane = lax.broadcasted_iota(jnp.int32, rows[0][0].shape, 1)
+    bit = 1
+    while bit < count:
+        step = bit * width
+        keep = (lane // step) % 2 == 0 if step < LANES else None
+        for f in range(count):
+            if f & bit:
+                continue
+            first, second = rows[f], rows[f | bit]
+            if step < LANES:
+                new_first = [
+                    jnp.where(keep, a, pltpu.roll(b, step, 1)) for a, b in zip(first, second)
+                ]
+                new_second = [
+                    jnp.where(keep, pltpu.roll(a, LANES - step, 1), b)
+                    for a, b in zip(first, second)
+                ]
+            else:
+                hop = step // LANES
+                new_first, new_second = list(first), list(second)
+                for h in range(len(first)):
+                    if h & hop:
+                        new_first[h] = second[h ^ hop]
+                    else:
+                        new_second[h] = first[h ^ hop]
+            rows[f], rows[f | bit] = new_first, new_second
+        bit *= 2
+    return rows
+
+
+def split(values):
+    high = values.astype(jnp.bfloat16)
+    return high, (values - high.astype(jnp.float32)).astype(jnp.bfloat16)
+
+
+def bf16_dot(left, right, dims=(((1,), (0,)), ((), ()))):
+    return lax.dot_general(left, right, dims, preferred_element_type=jnp.float32)
+
+
+def kernel(
+    n, chunks, guard_ref, train_ref, x_ref, table_high, table_low, twist_cos, twist_sin, perm_ref,
+    power_ref, stat_ref,
+    sent, got, mixed, cells, landed, padded, edges,
+    send_one, recv_one, send_two, recv_two, send_edge, recv_edge,
+):
+    me = lax.axis_index("pulse")
+    length, gates = x_ref.shape[1], x_ref.shape[2]
+    part = gates // n // chunks
+    halves = length // LANES
+    barrier = pltpu.get_barrier_semaphore()
+    for o in range(1, n):
+        pl.semaphore_signal(barrier, inc=1, device_id={"pulse": lax.rem(me + o, n)})
+    for p in range(2):
+        sent[:, :, p] = x_ref[p].T.reshape(n, chunks, part, length)
+    pl.semaphore_wait(barrier, n - 1)
+
+    def first_copy(c, o):
+        peer = lax.rem(me + o, n)
+        return pltpu.make_async_remote_copy(
+            src_ref=sent.at[peer, c], dst_ref=got.at[c, me],
+            send_sem=send_one.at[c, o], recv_sem=recv_one.at[c, o],
+            device_id={"pulse": peer},
+        )
+
+    def second_copy(c, o):
+        peer = lax.rem(me + o, n)
+        return pltpu.make_async_remote_copy(
+            src_ref=cells.at[peer, c], dst_ref=landed.at[me, c],
+            send_sem=send_two.at[c, o], recv_sem=recv_two.at[c, o],
+            device_id={"pulse": peer},
+        )
+
+    order = peer_order(n)
+    for c in range(chunks):
+        for o in order:
+            first_copy(c, o).start()
+    for c in range(chunks):
+        got[c, me] = sent[me, c]
+    gate_row = lax.broadcasted_iota(jnp.int32, (gates, gates), 0)
+    gate_col = lax.broadcasted_iota(jnp.int32, (gates, gates), 1)
+    offsets = jnp.abs(gate_row - gate_col)
+    guard, train = guard_ref[0], train_ref[0]
+    inside = ((offsets > guard) & (offsets <= guard + train)).astype(jnp.float32)
+    range_count = jnp.sum(inside, axis=0, keepdims=True)
+    band = inside.astype(jnp.bfloat16)
+
+    for c in range(chunks):
+        for o in order:
+            first_copy(c, o).wait_recv()
+        for r in range(0, part, ROWS):
+            for h in range(halves):
+                lanes = slice(h * LANES, (h + 1) * LANES)
+                spectra = butterflies(
+                    [
+                        (got[c, s, 0, r : r + ROWS, lanes], got[c, s, 1, r : r + ROWS, lanes])
+                        for s in range(n)
+                    ]
+                )
+                for f, (re, im) in enumerate(spectra):
+                    tc, ts = twist_cos[f : f + 1, lanes], twist_sin[f : f + 1, lanes]
+                    mixed[0, f, r : r + ROWS, lanes] = tc * re + ts * im
+                    mixed[1, f, r : r + ROWS, lanes] = tc * im - ts * re
+        high, low = split(mixed[...].reshape(2 * n * part, length))
+        both = (
+            bf16_dot(high, table_high[...])
+            + bf16_dot(low, table_high[...])
+            + bf16_dot(high, table_low[...])
+        ).reshape(2, n * part, 2 * length)
+        real = both[0, :, :length] + both[1, :, length:]
+        imag = both[1, :, :length] - both[0, :, length:]
+        power = (real * real + imag * imag).reshape(n, part, length)
+        rows = [
+            [power[f, :, h * LANES : (h + 1) * LANES] for h in range(halves)] for f in range(n)
+        ]
+        rows = swap_digits(rows, length // n)
+        for d in range(n):
+            for h in range(halves):
+                cells[d, c, :, h * LANES : (h + 1) * LANES] = rows[d][h]
+        for o in order:
+            second_copy(c, o).start()
+        landed[me, c] = cells[me, c]
+    for c in range(chunks):
+        for o in order:
+            second_copy(c, o).wait_recv()
+
+    columns = landed[...].reshape(gates, length)
+    powers = lax.dot_general(
+        perm_ref[...], columns, (((1,), (1,)), ((), ())),
+        precision=HIGHEST, preferred_element_type=jnp.float32,
+    )
+    power_ref[...] = powers
+    edges[0] = powers[:ROWS]
+    edges[1] = powers[length - ROWS :]
+    above, below = lax.rem(me + 1, n), lax.rem(me + n - 1, n)
+    tail_copy = pltpu.make_async_remote_copy(
+        src_ref=edges.at[1], dst_ref=edges.at[2],
+        send_sem=send_edge.at[0], recv_sem=recv_edge.at[0], device_id={"pulse": above},
+    )
+    head_copy = pltpu.make_async_remote_copy(
+        src_ref=edges.at[0], dst_ref=edges.at[3],
+        send_sem=send_edge.at[1], recv_sem=recv_edge.at[1], device_id={"pulse": below},
+    )
+    tail_copy.start()
+    head_copy.start()
+    high, low = split(powers)
+    range_sum = bf16_dot(high, band) + bf16_dot(low, band)
+    padded[ROWS : ROWS + length] = powers
+    tail_copy.wait_recv()
+    head_copy.wait_recv()
+    padded[:ROWS] = edges[2]
+    padded[ROWS + length :] = edges[3]
+    total = range_sum
+    for d in range(GUARD_BINS + 1, GUARD_BINS + TRAIN_BINS + 1):
+        total = total + padded[ROWS + d : ROWS + d + length] + padded[ROWS - d : ROWS - d + length]
+    noise = total / (range_count + 2.0 * TRAIN_BINS)
+    stat_ref[...] = powers / (noise + 1.0)
+    tail_copy.wait_send()
+    head_copy.wait_send()
+    for c in range(chunks):
+        for o in order:
+            first_copy(c, o).wait_send()
+            second_copy(c, o).wait_send()
+
+
+def peer_order(n):
+    return list(range(1, n))
+
+
+def tables(n, length):
+    lane = np.arange(length)
+    turn = 2 * np.pi * (np.outer(lane, lane) % length) / length
+    both = np.concatenate([np.cos(turn), np.sin(turn)], axis=1).astype(np.float32)
+    high = both.astype(jnp.bfloat16)
+    low = (both - high.astype(np.float32)).astype(jnp.bfloat16)
+    twist = 2 * np.pi * np.outer(np.arange(n), lane) / (n * length)
+    scale = 1.0 / np.sqrt(n * length)
+    perm = np.zeros((length, length), np.float32)
+    width = length // n
+    for f in range(n):
+        for e in range(width):
+            perm[f + n * e, f * width + e] = 1.0
+    return (
+        high, low,
+        (np.cos(twist) * scale).astype(np.float32),
+        (np.sin(twist) * scale).astype(np.float32),
+        perm,
+    )
+
+
+def kernel_shards(echoes, guard_gates, train_gates):
+    n = lax.axis_size("pulse")
+    length, gates = echoes.shape[1], echoes.shape[2]
+    chunks = CHUNKS if gates % (n * ROWS * CHUNKS) == 0 else 1
+    part = gates // n // chunks
+    smem = pl.BlockSpec(memory_space=pltpu.SMEM)
+    vmem = pl.BlockSpec(memory_space=pltpu.VMEM)
+    out = jax.ShapeDtypeStruct((length, gates), jnp.float32)
+    dma = pltpu.SemaphoreType.DMA
+    return pl.pallas_call(
+        functools.partial(kernel, n, chunks),
+        out_shape=(out, out),
+        in_specs=[smem, smem] + [vmem] * 6,
+        out_specs=(vmem, vmem),
+        scratch_shapes=[
+            pltpu.VMEM((n, chunks, 2, part, length), jnp.float32),
+            pltpu.VMEM((chunks, n, 2, part, length), jnp.float32),
+            pltpu.VMEM((2, n, part, length), jnp.float32),
+            pltpu.VMEM((n, chunks, part, length), jnp.float32),
+            pltpu.VMEM((n, chunks, part, length), jnp.float32),
+            pltpu.VMEM((length + 2 * ROWS, gates), jnp.float32),
+            pltpu.VMEM((4, ROWS, gates), jnp.float32),
+            dma((chunks, n)), dma((chunks, n)), dma((chunks, n)), dma((chunks, n)),
+            dma((2,)), dma((2,)),
+        ],
+        compiler_params=pltpu.CompilerParams(
+            collective_id=0, has_side_effects=True, vmem_limit_bytes=60 * 2**20
+        ),
+    )(guard_gates, train_gates, echoes, *(jnp.asarray(t) for t in tables(n, length)))
+
+
+CHUNKS = 3
+
+
+def shards(echoes, guard_gates, train_gates):
+    n = lax.axis_size("pulse")
+    length, gates = echoes.shape[1], echoes.shape[2]
+    fits = length % LANES == 0 and length % n == 0 and n > 2 and gates % (n * ROWS) == 0
+    fits = fits and n & (n - 1) == 0 and length & (length - 1) == 0 and LANES % (length // n) == 0
+    if fits and GUARD_BINS + TRAIN_BINS <= ROWS:
+        return kernel_shards(echoes, guard_gates, train_gates)
+    return generic_shards(echoes, guard_gates, train_gates)
+
+
 def solution(mesh):
     return jax.shard_map(
         shards,

time: 129 us -> 74.6 us (0.58)
  Pallas kernels: 0 us -> 69.4 us
  waiting for transfers between devices: 54.1 us -> 0 us
  local copies, waits for them, and re-layouts: 28.2 us -> 3.02 us
  starting transfers between devices: 20.6 us -> 0 us
  matrix products: 18.6 us -> 0 us
  other arithmetic: 5 us -> 0 us
    pallas_call x0 -> x1, Pallas kernels: none -> 69.4 us  [kernel_shards(): pl.pallas_call(functools.partial(kernel, n, chunks), out_shape=(out, out)...]
    all_to_all x2 -> x0, waiting for transfers between devices: 48.5 us -> none  [the longest x1 31.7 us: shards(): lax.all_to_all(echoes, 'pulse', split_axis=2, concat_axis=1, tiled=True)]
    dot_general x9 -> x0, matrix products: 18.6 us -> none  [the longest x8 15.5 us: product(): jnp.dot(left, right, precision=lax.Precision.HIGHEST, preferred_element_t...]
    all_to_all x2 -> x0, starting transfers between devices: 16.5 us -> none  [the longest x1 9.12 us: shards(): lax.all_to_all(columns, 'pulse', split_axis=0, concat_axis=1, tiled=True)]
    reshape x4 -> x0, local copies, waits for them, and re-layouts: 9.51 us -> none  [the longest x1 3.08 us: factored_powers(): (product(cos_first, real_in) + product(sin_first, imag_in)).reshape(first...]
    ppermute x2 -> x0, waiting for transfers between devices: 5.64 us -> none  [the longest x1 4.6 us: padded_2(): lax.ppermute(tail, axis, [(i, (i + 1) % count) for i in range(count)])]
    another operation x2 -> x0, local copies, waits for them, and re-layouts: 4.43 us -> none  [the longest x1 2.66 us: factored_powers(): real_in = samples[0].reshape(first_radix, second_radix * width)]
    transpose x1 -> x0, other arithmetic: 4.25 us -> none  [factored_powers(): jnp.transpose(imag_two, (1, 0, 2))]
  transfers between devices with their start and end apart: 4 -> 0, of which waited for: 4 -> 0; matrix products, arithmetic and copies ran while one was open for 1% -> 0% of each run, Pallas kernels for 0% -> 0%
where the time goes in v1:
time: 74.6 us; the launch traced here: 74.4 us
  Pallas kernels  69.4 us (93%)
  local copies, waits for them, and re-layouts  3.02 us (4%)
  between operations  1.94 us (3%)
    pallas_call x1, Pallas kernels, kernel_shards(): pl.pallas_call(functools.partial(kernel, n, chunks), out_shape=(out, out)...  69.4 us
    unnamed x4, local copies, waits for them, and re-layouts  3.02 us

profile of v1, /device:TPU:0, one launch (start us, length us, event | category | flops | bytes accessed | tf_op | source)
XLA Modules:
  0.0 74.4 jit_solution(8526451253386575399)
XLA Ops:
  1.9 69.4 %shard_map.95 = (f32[256,768]{1,0:T(8,128)}, f32[256,768]{1,0:T(8,128)}) custom-call(s32[1]{0:T(128)S(6)} %copy.12.guard_ref, s32[1]{0:T(128)S(6)} %copy.13.train_ref, f32[2,256,768]{2,1,0:T(8,128)} %x_ref.1, bf16[256,512]{1,0:T(8,128)(2,1)} %constant.10.clone.table_high, bf16[256,512]{1,0:T(8,128)(2,1)} %constant.11.clone.table_low, ...), custom_call_target="tpu_custom_call" | custom-call | tf_op jit(solution)/shard_map/pallas_call | solution.py:334
  71.3 0.0 copy-start
  71.4 2.1 %copy.14 = f32[256,768]{1,0:T(8,128)} copy(f32[256,768]{1,0:T(8,128)} %get-tuple-element.4) | data formatting | bytes 1572864
  73.5 0.0 copy-done
  73.5 0.9 %copy.15 = f32[256,768]{1,0:T(8,128)} copy(f32[256,768]{1,0:T(8,128)S(1)} %copy-done) | data formatting | bytes 1572864
Async XLA Ops:
  71.3 2.1 %copy-start = (f32[256,768]{1,0:T(8,128)S(1)}, f32[256,768]{1,0:T(8,128)}, u32[]{:S(2)}) copy-start(f32[256,768]{1,0:T(8,128)} %get-tuple-element.5) | copy-start | bytes 2359300

commit v2 on v1

--- a/solution.py
+++ b/solution.py
@@ -173,10 +173,11 @@
 
 
 def kernel(
-    n, chunks, guard_ref, train_ref, x_ref, table_high, table_low, twist_cos, twist_sin, perm_ref,
+    n, chunks, guard_ref, train_ref, x_any, high_any, low_any, cos_any, sin_any, perm_any,
     power_ref, stat_ref,
     sent, got, mixed, cells, landed, padded, edges,
-    send_one, recv_one, send_two, recv_two, send_edge, recv_edge,
+    x_ref, table_high, table_low, twist_cos, twist_sin, perm_ref,
+    send_one, recv_one, send_two, recv_two, send_edge, recv_edge, load,
 ):
     me = lax.axis_index("pulse")
     length, gates = x_ref.shape[1], x_ref.shape[2]
@@ -185,12 +186,22 @@
     barrier = pltpu.get_barrier_semaphore()
     for o in range(1, n):
         pl.semaphore_signal(barrier, inc=1, device_id={"pulse": lax.rem(me + o, n)})
+    loads = [pltpu.make_async_copy(x_any.at[p], x_ref.at[p], load.at[p]) for p in range(2)]
+    pairs = (
+        (high_any, table_high), (low_any, table_low), (cos_any, twist_cos), (sin_any, twist_sin),
+        (perm_any, perm_ref),
+    )
+    for i, (source, target) in enumerate(pairs):
+        loads.append(pltpu.make_async_copy(source, target, load.at[2 + i]))
+    for copy in loads:
+        copy.start()
     for p in range(2):
+        loads[p].wait()
         sent[:, :, p] = x_ref[p].T.reshape(n, chunks, part, length)
     pl.semaphore_wait(barrier, n - 1)
 
     def first_copy(c, o):
-        peer = lax.rem(me + o, n)
+        peer = partner(me, o)
         return pltpu.make_async_remote_copy(
             src_ref=sent.at[peer, c], dst_ref=got.at[c, me],
             send_sem=send_one.at[c, o], recv_sem=recv_one.at[c, o],
@@ -198,7 +209,7 @@
         )
 
     def second_copy(c, o):
-        peer = lax.rem(me + o, n)
+        peer = partner(me, o)
         return pltpu.make_async_remote_copy(
             src_ref=cells.at[peer, c], dst_ref=landed.at[me, c],
             send_sem=send_two.at[c, o], recv_sem=recv_two.at[c, o],
@@ -211,6 +222,8 @@
             first_copy(c, o).start()
     for c in range(chunks):
         got[c, me] = sent[me, c]
+    for copy in loads[2:]:
+        copy.wait()
     gate_row = lax.broadcasted_iota(jnp.int32, (gates, gates), 0)
     gate_col = lax.broadcasted_iota(jnp.int32, (gates, gates), 1)
     offsets = jnp.abs(gate_row - gate_col)
@@ -297,8 +310,17 @@
             second_copy(c, o).wait_send()
 
 
+def partner(me, offset):
+    peer, bit = me, 1
+    while bit <= offset:
+        if offset & bit:
+            peer = peer + bit * (1 - 2 * lax.rem(lax.div(me, bit), 2))
+        bit *= 2
+    return peer
+
+
 def peer_order(n):
-    return list(range(1, n))
+    return list(range(n - 1, 0, -1))
 
 
 def tables(n, length):
@@ -334,7 +356,7 @@
     return pl.pallas_call(
         functools.partial(kernel, n, chunks),
         out_shape=(out, out),
-        in_specs=[smem, smem] + [vmem] * 6,
+        in_specs=[smem, smem] + [pl.BlockSpec(memory_space=pl.ANY)] * 6,
         out_specs=(vmem, vmem),
         scratch_shapes=[
             pltpu.VMEM((n, chunks, 2, part, length), jnp.float32),
@@ -344,16 +366,22 @@
             pltpu.VMEM((n, chunks, part, length), jnp.float32),
             pltpu.VMEM((length + 2 * ROWS, gates), jnp.float32),
             pltpu.VMEM((4, ROWS, gates), jnp.float32),
+            pltpu.VMEM(echoes.shape, jnp.float32),
+            pltpu.VMEM((length, 2 * length), jnp.bfloat16),
+            pltpu.VMEM((length, 2 * length), jnp.bfloat16),
+            pltpu.VMEM((n, length), jnp.float32),
+            pltpu.VMEM((n, length), jnp.float32),
+            pltpu.VMEM((length, length), jnp.float32),
             dma((chunks, n)), dma((chunks, n)), dma((chunks, n)), dma((chunks, n)),
-            dma((2,)), dma((2,)),
+            dma((2,)), dma((2,)), dma((7,)),
         ],
         compiler_params=pltpu.CompilerParams(
-            collective_id=0, has_side_effects=True, vmem_limit_bytes=60 * 2**20
+            collective_id=0, has_side_effects=True, vmem_limit_bytes=20 * 2**20
         ),
-    )(guard_gates, train_gates, echoes, *(jnp.asarray(t) for t in tables(n, length)))
-
-
-CHUNKS = 3
+    )(guard_gates, train_gates, *(pltpu.with_memory_space_constraint(t, pltpu.HBM) for t in (echoes, *(jnp.asarray(t) for t in tables(n, length)))))
+
+
+CHUNKS = 2
 
 
 def shards(echoes, guard_gates, train_gates):

time: 74.6 us -> 68.9 us (0.924)
  Pallas kernels: 69.4 us -> 65 us
  local copies, waits for them, and re-layouts: 3.02 us -> 1.76 us
    pallas_call x1, Pallas kernels: 69.4 us -> 65 us  [kernel_shards(): pl.pallas_call(functools.partial(kernel, n, chunks), out_shape=(out, out)...]
    unnamed x4 -> x2, local copies, waits for them, and re-layouts: 3.02 us -> 1.76 us
where the time goes in v2:
time: 68.9 us; the launch traced here: 68.7 us
  Pallas kernels  65 us (94%)
  between operations  1.93 us (3%)
  local copies, waits for them, and re-layouts  1.76 us (3%)
    pallas_call x1, Pallas kernels, kernel_shards(): pl.pallas_call(functools.partial(kernel, n, chunks), out_shape=(out, out)...  65 us
    unnamed x2, local copies, waits for them, and re-layouts  1.76 us

profile of v2, /device:TPU:0, one launch (start us, length us, event | category | flops | bytes accessed | tf_op | source)
XLA Modules:
  0.0 68.7 jit_solution(6943725962160265038)
XLA Ops:
  1.9 65.0 %shard_map.95 = (f32[256,768]{1,0:T(8,128)S(1)}, f32[256,768]{1,0:T(8,128)S(1)}) custom-call(s32[1]{0:T(128)S(6)} %copy.12.guard_ref, s32[1]{0:T(128)S(6)} %copy.13.train_ref, f32[2,256,768]{2,1,0:T(8,128)} %x_any.1, bf16[256,512]{1,0:T(8,128)(2,1)} %constant.10.clone.high_any, bf16[256,512]{1,0:T(8,128)(2,1)} %constant.11.clone.low_any, ...), custom_call_target="tpu_custom_call" | custom-call | tf_op jit(solution)/shard_map/pallas_call | solution.py:356
  66.9 0.9 %copy.14 = f32[256,768]{1,0:T(8,128)} copy(f32[256,768]{1,0:T(8,128)S(1)} %get-tuple-element.4) | data formatting | bytes 1572864
  67.8 0.9 %copy.15 = f32[256,768]{1,0:T(8,128)} copy(f32[256,768]{1,0:T(8,128)S(1)} %get-tuple-element.5) | data formatting | bytes 1572864

commit v3 on v2

--- a/solution.py
+++ b/solution.py
@@ -172,6 +172,13 @@
     return lax.dot_general(left, right, dims, preferred_element_type=jnp.float32)
 
 
+def rows_of(picks, columns):
+    return lax.dot_general(
+        picks, columns, (((1,), (1,)), ((), ())),
+        precision=HIGHEST, preferred_element_type=jnp.float32,
+    )
+
+
 def kernel(
     n, chunks, guard_ref, train_ref, x_any, high_any, low_any, cos_any, sin_any, perm_any,
     power_ref, stat_ref,
@@ -184,8 +191,8 @@
     part = gates // n // chunks
     halves = length // LANES
     barrier = pltpu.get_barrier_semaphore()
-    for o in range(1, n):
-        pl.semaphore_signal(barrier, inc=1, device_id={"pulse": lax.rem(me + o, n)})
+    for o in peer_order(n):
+        pl.semaphore_signal(barrier, inc=1, device_id={"pulse": partner(me, o)})
     loads = [pltpu.make_async_copy(x_any.at[p], x_ref.at[p], load.at[p]) for p in range(2)]
     pairs = (
         (high_any, table_high), (low_any, table_low), (cos_any, twist_cos), (sin_any, twist_sin),
@@ -272,13 +279,10 @@
             second_copy(c, o).wait_recv()
 
     columns = landed[...].reshape(gates, length)
-    powers = lax.dot_general(
-        perm_ref[...], columns, (((1,), (1,)), ((), ())),
-        precision=HIGHEST, preferred_element_type=jnp.float32,
-    )
-    power_ref[...] = powers
-    edges[0] = powers[:ROWS]
-    edges[1] = powers[length - ROWS :]
+    ends = jnp.concatenate([perm_ref[:ROWS], perm_ref[length - ROWS :]])
+    ends = rows_of(ends, columns)
+    edges[0] = ends[:ROWS]
+    edges[1] = ends[ROWS:]
     above, below = lax.rem(me + 1, n), lax.rem(me + n - 1, n)
     tail_copy = pltpu.make_async_remote_copy(
         src_ref=edges.at[1], dst_ref=edges.at[2],
@@ -290,18 +294,27 @@
     )
     tail_copy.start()
     head_copy.start()
+    powers = rows_of(perm_ref[...], columns)
+    power_ref[...] = powers
     high, low = split(powers)
     range_sum = bf16_dot(high, band) + bf16_dot(low, band)
     padded[ROWS : ROWS + length] = powers
+
+    def finish(first, last):
+        total = range_sum[first:last]
+        for d in range(GUARD_BINS + 1, GUARD_BINS + TRAIN_BINS + 1):
+            for move in (d, -d):
+                total = total + padded[ROWS + first + move : ROWS + last + move]
+        noise = total / (range_count + 2.0 * TRAIN_BINS)
+        stat_ref[first:last] = powers[first:last] / (noise + 1.0)
+
+    finish(ROWS, length - ROWS)
     tail_copy.wait_recv()
     head_copy.wait_recv()
     padded[:ROWS] = edges[2]
     padded[ROWS + length :] = edges[3]
-    total = range_sum
-    for d in range(GUARD_BINS + 1, GUARD_BINS + TRAIN_BINS + 1):
-        total = total + padded[ROWS + d : ROWS + d + length] + padded[ROWS - d : ROWS - d + length]
-    noise = total / (range_count + 2.0 * TRAIN_BINS)
-    stat_ref[...] = powers / (noise + 1.0)
+    finish(0, ROWS)
+    finish(length - ROWS, length)
     tail_copy.wait_send()
     head_copy.wait_send()
     for c in range(chunks):
@@ -353,7 +366,7 @@
     vmem = pl.BlockSpec(memory_space=pltpu.VMEM)
     out = jax.ShapeDtypeStruct((length, gates), jnp.float32)
     dma = pltpu.SemaphoreType.DMA
-    return pl.pallas_call(
+    results = pl.pallas_call(
         functools.partial(kernel, n, chunks),
         out_shape=(out, out),
         in_specs=[smem, smem] + [pl.BlockSpec(memory_space=pl.ANY)] * 6,
@@ -379,6 +392,25 @@
             collective_id=0, has_side_effects=True, vmem_limit_bytes=20 * 2**20
         ),
     )(guard_gates, train_gates, *(pltpu.with_memory_space_constraint(t, pltpu.HBM) for t in (echoes, *(jnp.asarray(t) for t in tables(n, length)))))
+    return pl.pallas_call(
+        write_out,
+        out_shape=(out, out),
+        in_specs=[vmem] * 2,
+        out_specs=(pl.BlockSpec(memory_space=pl.ANY),) * 2,
+        scratch_shapes=[dma((2,))],
+        compiler_params=pltpu.CompilerParams(vmem_limit_bytes=8 * 2**20),
+    )(*results)
+
+
+def write_out(power_in, stat_in, power_out, stat_out, done):
+    copies = [
+        pltpu.make_async_copy(power_in, power_out, done.at[0]),
+        pltpu.make_async_copy(stat_in, stat_out, done.at[1]),
+    ]
+    for copy in copies:
+        copy.start()
+    for copy in copies:
+        copy.wait()
 
 
 CHUNKS = 2

time: 68.9 us -> 67 us (0.972)
  local copies, waits for them, and re-layouts: 1.76 us -> 0 us
    unnamed x2 -> x0, local copies, waits for them, and re-layouts: 1.76 us -> none
    pallas_call x1, Pallas kernels: 65 us -> 63.8 us  [kernel_shards(): pl.pallas_call(functools.partial(kernel, n, chunks), out_shape=(out, out)...]
    pallas_call x0 -> x1, Pallas kernels: none -> 1.16 us  [kernel_shards(): pl.pallas_call(write_out, out_shape=(out, out), in_specs=[vmem] * 2, out_...]
where the time goes in v3:
time: 67 us; the launch traced here: 66.9 us
  Pallas kernels  65 us (97%)
  between operations  1.93 us (3%)
    pallas_call x1, Pallas kernels, kernel_shards(): pl.pallas_call(functools.partial(kernel, n, chunks), out_shape=(out, out)...  63.8 us

profile of v3, /device:TPU:0, one launch (start us, length us, event | category | flops | bytes accessed | tf_op | source)
XLA Modules:
  0.0 66.9 jit_solution(16797634574192058326)
XLA Ops:
  1.9 63.8 %shard_map.95 = (f32[256,768]{1,0:T(8,128)S(1)}, f32[256,768]{1,0:T(8,128)S(1)}) custom-call(s32[1]{0:T(128)S(6)} %copy.10.guard_ref, s32[1]{0:T(128)S(6)} %copy.11.train_ref, f32[2,256,768]{2,1,0:T(8,128)} %x_any.1, bf16[256,512]{1,0:T(8,128)(2,1)} %constant.10.clone.high_any, bf16[256,512]{1,0:T(8,128)(2,1)} %constant.11.clone.low_any, ...), custom_call_target="tpu_custom_call" | custom-call | tf_op jit(solution)/shard_map/pallas_call | solution.py:369
  65.7 1.2 %shard_map.96 = (f32[256,768]{1,0:T(8,128)}, f32[256,768]{1,0:T(8,128)}) custom-call(f32[256,768]{1,0:T(8,128)S(1)} %get-tuple-element.4.power_in, f32[256,768]{1,0:T(8,128)S(1)} %get-tuple-element.5.stat_in), custom_call_target="tpu_custom_call" | custom-call | tf_op jit(solution)/shard_map/pallas_call | solution.py:395

commit v4 on v3

--- a/solution.py
+++ b/solution.py
@@ -333,7 +333,9 @@
 
 
 def peer_order(n):
-    return list(range(n - 1, 0, -1))
+    half, quarter = n // 2, n // 4
+    near, far = range(half - 1, quarter - 1, -1), range(n - 1, half - 1, -1)
+    return [*near, *far, *range(quarter - 1, 0, -1)]
 
 
 def tables(n, length):

time: 67 us -> 67.6 us (level)
  no operation moved by 1% of the time
where the time goes in v4:
time: 67.6 us; the launch traced here: 67.4 us
  Pallas kernels  65.5 us (97%)
  between operations  1.93 us (3%)
    pallas_call x1, Pallas kernels, kernel_shards(): pl.pallas_call(functools.partial(kernel, n, chunks), out_shape=(out, out)...  64.3 us

profile of v4, /device:TPU:0, one launch (start us, length us, event | category | flops | bytes accessed | tf_op | source)
XLA Modules:
  0.0 67.4 jit_solution(8127391124339650010)
XLA Ops:
  1.9 64.3 %shard_map.95 = (f32[256,768]{1,0:T(8,128)S(1)}, f32[256,768]{1,0:T(8,128)S(1)}) custom-call(s32[1]{0:T(128)S(6)} %copy.10.guard_ref, s32[1]{0:T(128)S(6)} %copy.11.train_ref, f32[2,256,768]{2,1,0:T(8,128)} %x_any.1, bf16[256,512]{1,0:T(8,128)(2,1)} %constant.10.clone.high_any, bf16[256,512]{1,0:T(8,128)(2,1)} %constant.11.clone.low_any, ...), custom_call_target="tpu_custom_call" | custom-call | tf_op jit(solution)/shard_map/pallas_call | solution.py:371
  66.3 1.2 %shard_map.96 = (f32[256,768]{1,0:T(8,128)}, f32[256,768]{1,0:T(8,128)}) custom-call(f32[256,768]{1,0:T(8,128)S(1)} %get-tuple-element.4.power_in, f32[256,768]{1,0:T(8,128)S(1)} %get-tuple-element.5.stat_in), custom_call_target="tpu_custom_call" | custom-call | tf_op jit(solution)/shard_map/pallas_call | solution.py:397
